TPU v7x, 32 devices: a whole 2x2x4 slice. The times are simulated.
32 devices in a mesh: groups: 2 (over y), blk: 4 (over z), tile: 2 (over x), sub: 2 (over core).
Axes of the slice: x: 2, y: 2, z: 4, core: 2. Of those that a mesh axis runs over, the one named last changes fastest.
Arguments:
- raw_desc: bfloat16 [4096, 1536], P(('groups', 'blk', 'tile')), parts along dimension 0, may hold values from -11 to 11
- desc_mean: float32 [1536], replicated, may hold values from -6 to 6
- whitening: bfloat16 [1536, 256], P(None, 'sub'), may hold values from -0.15625 to 0.15625
Outputs:
- augmented: float32 [4096, 256], P(('groups', 'blk', 'tile'), 'sub'), parts along dimension 0
There are 2 independent parts, one for each index of `groups`. A program takes and returns all parts, laid end to end along the dimension named above; an argument that names none is the same for every part. Nothing has to cross between parts.
All inputs are finite; a program needn't handle non-finite values.
Results may differ from a plain program's by a relative error of at most 0.0055.
The roundings to bfloat16 on the way count: a program that leaves them out, or rounds other values in their place, can miss the bound.
Values may be sent and summed in bfloat16 or wider, within the bound.
A program may use at most 128 MiB of HBM per device.

v0:
```python
import jax
import jax.numpy as jnp
from jax import lax
from jax.sharding import PartitionSpec as P

beta = 0.125
lowest = -1e30


def merged_2(value, axis, combine):
    everything = jax.tree.map(lambda part: lax.all_gather(part, axis), value)
    leading = jax.tree.map(lambda part: part[0], everything)

    def hop(k, so_far):
        return combine(so_far, jax.tree.map(lambda part: part[k], everything))

    return lax.fori_loop(1, lax.axis_size(axis), hop, leading)


def local(raw_desc, desc_mean, whitening):
    rows = raw_desc.shape[0]
    centred = (raw_desc.astype(jnp.float32) - desc_mean).astype(jnp.bfloat16)
    half = jnp.dot(centred, whitening, preferred_element_type=jnp.float32).astype(jnp.bfloat16)
    width = half.shape[1]
    own = lax.all_gather(half, "sub", axis=1, tiled=True)
    queries = lax.all_gather(own, "tile", axis=0, tiled=True)
    tiles = lax.axis_size("tile")
    tile_id = lax.axis_index("tile")
    blk_id = lax.axis_index("blk")
    sub_id = lax.axis_index("sub")
    low_col = sub_id * width
    query_index = blk_id * (tiles * rows) + jnp.arange(queries.shape[0], dtype=jnp.int32)
    count = queries.shape[0]
    piece = lax.all_gather(own, "blk", axis=0, tiled=True)
    run_max = jnp.full((count,), lowest, jnp.float32)
    keys = piece.shape[0]
    scores = beta * lax.dot_general(
        queries, piece, (((1,), (1,)), ((), ())), preferred_element_type=jnp.float32
    )
    position = jnp.arange(keys, dtype=jnp.int32)
    key_index = (position // rows * tiles + tile_id) * rows + position % rows
    masked = query_index[:, None] == key_index[None, :]
    scores = jnp.where(masked, lowest, scores)
    new_max = jnp.maximum(run_max, jnp.max(scores, axis=1))
    expo = jnp.where(masked, 0.0, jnp.exp(scores - new_max[:, None]))
    values = lax.dynamic_slice_in_dim(piece, low_col, width, 1)
    added = jnp.dot(expo.astype(jnp.bfloat16), values, preferred_element_type=jnp.float32)
    total = jnp.sum(expo, axis=1)

    def combine(first, second):
        top = jnp.maximum(first[0], second[0])
        scale_one = jnp.exp(first[0] - top)
        scale_two = jnp.exp(second[0] - top)
        return (
            top,
            first[1] * scale_one + second[1] * scale_two,
            first[2] * scale_one[:, None] + second[2] * scale_two[:, None],
        )

    merged = merged_2((new_max, total, added), "tile", combine)
    row_start = tile_id * rows
    own_total = lax.dynamic_slice_in_dim(merged[1], row_start, rows, 0)
    own_summed = lax.dynamic_slice_in_dim(merged[2], row_start, rows, 0)
    mixed = half.astype(jnp.float32) + own_summed / own_total[:, None]
    squares = lax.psum(jnp.sum(mixed * mixed, axis=1), "sub")
    return mixed * lax.rsqrt(squares + 1e-06)[:, None]


def solution(mesh):
    return jax.shard_map(
        local,
        mesh=mesh,
        in_specs=(P(("groups", "blk", "tile"), None), P(), P(None, "sub")),
        out_specs=P(("groups", "blk", "tile"), "sub"),
        check_vma=False,
    )
```

profile of v0, /device:TPU:0, one launch (start us, length us, event | category | flops | bytes accessed | tf_op | source)
XLA Modules:
  0.0 49.0 jit_solution(18015833948920306299)
XLA Ops:
  0.0 0.0 copy-start
  0.0 1.0 %copy-done = bf16[1536,128]{1,0:T(8,128)(2,1)S(1)} copy-done((bf16[1536,128]{1,0:T(8,128)(2,1)S(1)}, bf16[1536,128]{1,0:T(8,128)(2,1)}, u32[]{:S(2)}) %copy-start) | copy-done | bytes 393240
  1.0 1.5 %convolution_convert_fusion = bf16[256,128]{0,1:T(8,128)(2,1)S(1)} fusion(bf16[1536,128]{1,0:T(8,128)(2,1)S(1)} %copy-done, bf16[256,1536]{1,0:T(8,128)(2,1)} %param.3, f32[1536]{0:T(1024)} %param.4), kind=kOutput, calls=%fused_computation.6 | convolution fusion | flops 101875712 | bytes 1251328 | tf_op jit(solution)/shard_map/dot_general | solution.py:23
  2.5 2.0 %all_gather.25 = bf16[256,256]{0,1:T(8,128)(2,1)S(1)} all-gather(bf16[256,128]{0,1:T(8,128)(2,1)S(1)} %convolution_convert_fusion), channel_id=1, replica_groups=mesh['groups'=2,'blk'=4,'tile'=2,'sub'=2] {'sub'}, dimensions={1}, use_global_device_ids=true | all-gather | bytes 196608 | tf_op jit(solution)/shard_map/all_gather | solution.py:25
  4.6 7.3 %all_gather.26 = bf16[512,256]{0,1:T(8,128)(2,1)S(1)} all-gather(bf16[256,256]{0,1:T(8,128)(2,1)S(1)} %all_gather.25), channel_id=1, replica_groups=mesh['groups'=2,'blk'=4,'tile'=2,'sub'=2] {'tile'}, dimensions={0}, use_global_device_ids=true | all-gather | bytes 393216 | tf_op jit(solution)/shard_map/all_gather | solution.py:26
  11.8 15.7 %all_gather.27 = bf16[1024,256]{0,1:T(8,128)(2,1)S(1)} all-gather(bf16[256,256]{0,1:T(8,128)(2,1)S(1)} %all_gather.25), channel_id=1, replica_groups=mesh['groups'=2,'blk'=4,'tile'=2,'sub'=2] {'blk'}, dimensions={0}, use_global_device_ids=true | all-gather | bytes 655360 | tf_op jit(solution)/shard_map/all_gather | solution.py:34
  27.5 0.6 %fusion = (f32[512]{0:T(512)S(1)}, f32[512,1024]{1,0:T(8,128)S(1)}) fusion(s32[1024]{0:T(1024)S(1)} %fusion.19, s32[512]{0:T(512)S(1)} %iota_add_fusion, bf16[512,256]{0,1:T(8,128)(2,1)S(1)} %all_gather.26, bf16[1024,256]{0,1:T(8,128)(2,1)S(1)} %all_gather.27), kind=kOutput, calls=%fused_computation.2 | convolution fusion | flops 270532096 | bytes 2891776 | tf_op jit(solution)/shard_map/dot_general | solution.py:37
  28.1 0.8 %fusion.3 = f32[512,128]{0,1:T(8,128)S(1)} fusion(f32[512,1024]{1,0:T(8,128)S(1)} %get-tuple-element.41, f32[512]{0:T(512)S(1)} %broadcast_maximum_fusion, s32[1024]{0:T(1024)S(1)} %fusion.19, s32[512]{0:T(512)S(1)} %iota_add_fusion, bf16[1024,256]{0,1:T(8,128)(2,1)S(1)} %all_gather.27, s32[]{:T(128)S(6)} %select_n.42), kind=kOutput, calls=%fused_computation.7 | convolution fusion | flops 137363456 | bytes 2629636 | tf_op jit(solution)/shard_map/dot_general | solution.py:47
  28.9 0.7 %fusion.1 = f32[512]{0:T(512)S(1)} fusion(f32[512,1024]{1,0:T(8,128)S(1)} %get-tuple-element.41, f32[512]{0:T(512)S(1)} %broadcast_maximum_fusion, s32[1024]{0:T(1024)S(1)} %fusion.19, s32[512]{0:T(512)S(1)} %iota_add_fusion), kind=kLoop, calls=%fused_computation.4 | loop fusion | flops 3145216 | bytes 2107392 | tf_op jit(solution)/shard_map/reduce_sum | solution.py:48
  29.6 4.4 %all-gather.3 = f32[2,1,512]{2,1,0:T(1,128)S(1)} all-gather(f32[1,1,512]{2,1,0:T(1,128)S(1)} %bitcast.9), channel_id=3, replica_groups=mesh['groups'=2,'blk'=4,'tile'=2,'sub'=2] {'tile'}, dimensions={0}, use_global_device_ids=true | all-gather | bytes 6144 | tf_op jit(solution)/shard_map/all_gather | solution.py:11
  34.0 4.4 %all-gather.4 = f32[2,1,512]{2,1,0:T(1,128)S(1)} all-gather(f32[1,1,512]{2,1,0:T(1,128)S(1)} %bitcast.10), channel_id=4, replica_groups=mesh['groups'=2,'blk'=4,'tile'=2,'sub'=2] {'tile'}, dimensions={0}, use_global_device_ids=true | all-gather | bytes 6144 | tf_op jit(solution)/shard_map/all_gather | solution.py:11
  38.4 0.1 dynamic_slice.26
  38.4 0.1 dynamic-slice
  38.5 0.1 dynamic-slice.1
  38.6 7.0 %all-gather = f32[1024,128]{0,1:T(8,128)S(1)} all-gather(f32[512,128]{0,1:T(8,128)S(1)} %fusion.3), channel_id=2, replica_groups=mesh['groups'=2,'blk'=4,'tile'=2,'sub'=2] {'tile'}, dimensions={0}, use_global_device_ids=true | all-gather | bytes 786432 | tf_op jit(solution)/shard_map/all_gather | solution.py:11
  45.7 0.1 multiply_reduce_fusion
  45.7 2.5 %psum.7 = f32[256]{0:T(256)S(1)} all-reduce(f32[256]{0:T(256)S(1)} %get-tuple-element.19), channel_id=1, replica_groups=mesh['groups'=2,'blk'=4,'tile'=2,'sub'=2] {'sub'}, use_global_device_ids=true, to_apply=%region_3.4 | all-reduce | flops 256 | bytes 2048 | tf_op jit(solution)/shard_map/psum | solution.py:65
  48.2 0.8 %copy.7 = f32[256,128]{1,0:T(8,128)} copy(f32[256,128]{0,1:T(8,128)S(1)} %broadcast_multiply_fusion) | data formatting | bytes 262144 | tf_op jit(solution)/shard_map/mul | solution.py:66
  (9 shorter events, 0.1 us)
Async XLA Ops:
  0.0 1.0 %copy-start = (bf16[1536,128]{1,0:T(8,128)(2,1)S(1)}, bf16[1536,128]{1,0:T(8,128)(2,1)}, u32[]{:S(2)}) copy-start(bf16[1536,128]{1,0:T(8,128)(2,1)} %param.5) | copy-start | bytes 1179652
where the time goes:
time: 49.2 us; the launch traced here: 49 us
  blocking collectives  43.3 us (88%)
  matrix products  2.86 us (6%)
  local copies, waits for them, and re-layouts  2 us (4%)
  other arithmetic  0.81 us (2%)
    all_gather x3, blocking collectives, merged_2(): everything = jax.tree.map(lambda part: lax.all_gather(part, axis), value)  15.8 us
    all_gather x1, blocking collectives, local(): piece = lax.all_gather(own, 'blk', axis=0, tiled=True)  15.7 us
    all_gather x1, blocking collectives, local(): queries = lax.all_gather(own, 'tile', axis=0, tiled=True)  7.29 us
    psum x1, blocking collectives, local(): squares = lax.psum(jnp.sum(mixed * mixed, axis=1), 'sub')  2.47 us
    all_gather x1, blocking collectives, local(): own = lax.all_gather(half, 'sub', axis=1, tiled=True)  2.04 us
    dot_general x1, matrix products, local(): jnp.dot(centred, whitening, preferred_element_type=jnp.float32)  1.51 us
    unnamed x2, local copies, waits for them, and re-layouts  0.98 us

commit v1 on v0

v1 whole, which is shorter than its diff:
```python
import functools

import jax
import jax.numpy as jnp
from jax import lax
from jax.experimental import pallas as pl
from jax.experimental.pallas import tpu as pltpu
from jax.sharding import PartitionSpec as P

beta = 0.125
lowest = -1e30
MESH = pl.DeviceIdType.MESH


def repeat(count, body):
    if count <= 8:
        for k in range(count):
            body(k)
    else:
        lax.fori_loop(0, count, lambda k, _: (body(k), 0)[1], 0)


def peer_of(me, k, count):
    if count == 4:
        if k == 0:
            return me + 1 - 2 * lax.rem(me, 2)
        if k == 1:
            return lax.rem(me + 2, 4)
        return 3 - me
    return lax.rem(me + k + 1, count)


def kernel(
    blks, tiles, chunks,
    raw_hbm, mean_ref, white_hbm, out_ref,
    raw, white, feats, keys, acc, stat, put_acc, put_stat, got_acc, got_stat,
    raw_sem, white_sem, pair_send, pair_recv, own_send, fwd_send, key_recv,
    part_send, part_recv,
):
    z, x, s = lax.axis_index("blk"), lax.axis_index("tile"), lax.axis_index("sub")
    other = 1 - s
    rows, width = feats.shape[1], feats.shape[2]
    part = rows // 2
    step = rows // chunks
    load_white = pltpu.make_async_copy(white_hbm, white, white_sem)
    load_white.start()
    loads = []
    for c in range(chunks):
        at = pl.ds(c * step, step)
        loads.append(pltpu.make_async_copy(raw_hbm.at[at], raw.at[at], raw_sem.at[c]))
        loads[-1].start()

    barrier = pltpu.get_barrier_semaphore()
    pl.semaphore_signal(barrier, inc=1, device_id={"sub": other}, device_id_type=MESH)

    def greet_z(k):
        for r in range(2):
            pl.semaphore_signal(
                barrier, inc=1, device_id={"blk": peer_of(z, k, blks), "sub": r},
                device_id_type=MESH,
            )

    def greet_x(k):
        for r in range(2):
            pl.semaphore_signal(
                barrier, inc=1, device_id={"tile": peer_of(x, k, tiles), "sub": r},
                device_id_type=MESH,
            )

    repeat(blks - 1, greet_z)
    repeat(tiles - 1, greet_x)

    def piece(r):
        return feats.at[s, pl.ds(r * part, part)]

    def slot(zz, xx):
        return zz * tiles + xx

    def own_to_z(k, r):
        return pltpu.make_async_remote_copy(
            piece(r), keys.at[slot(z, x), s], own_send.at[k, r], key_recv.at[slot(z, x), s],
            device_id={"blk": peer_of(z, k, blks), "sub": r}, device_id_type=MESH,
        )

    def own_to_x(k, r):
        return pltpu.make_async_remote_copy(
            piece(r), keys.at[slot(z, x), s], own_send.at[blks - 1 + k, r],
            key_recv.at[slot(z, x), s],
            device_id={"tile": peer_of(x, k, tiles), "sub": r}, device_id_type=MESH,
        )

    def forward(k, j, h):
        block = slot(peer_of(z, k, blks), x)
        return pltpu.make_async_remote_copy(
            keys.at[block, h], keys.at[block, h], fwd_send.at[k, j, h],
            key_recv.at[block, h],
            device_id={"tile": peer_of(x, j, tiles)}, device_id_type=MESH,
        )

    def pair(r):
        return pltpu.make_async_remote_copy(
            piece(r), piece(r), pair_send.at[r], pair_recv.at[r],
            device_id={"sub": other}, device_id_type=MESH,
        )

    mean = mean_ref[...].reshape(1, -1)
    load_white.wait()
    for c in range(chunks):
        loads[c].wait()
        at = pl.ds(c * step, step)
        centred = (raw[at, :].astype(jnp.float32) - mean).astype(jnp.bfloat16)
        half = jnp.dot(centred, white[...], preferred_element_type=jnp.float32)
        feats[s, at, :] = half.astype(jnp.bfloat16)
        if (c + 1) % (chunks // 2) == 0:
            r = (c + 1) // (chunks // 2) - 1
            if r == 0:
                pl.semaphore_wait(barrier, 1 + 2 * (blks - 1) + 2 * (tiles - 1))
            repeat(blks - 1, lambda k: own_to_z(k, r).start())
            repeat(tiles - 1, lambda k: own_to_x(k, r).start())
            pair(r).start()

    def arrived(block, h):
        pltpu.make_async_copy(
            keys.at[block, h], keys.at[block, h], key_recv.at[block, h]
        ).wait()

    def scores_of(k0, k1):
        nt = (((1,), (1,)), ((), ()))
        q = jnp.concatenate([feats[0], feats[1]], axis=1)
        kk = jnp.concatenate([k0, k1], axis=1)
        return beta * lax.dot_general(q, kk, nt, preferred_element_type=jnp.float32), kk

    def attend(block):
        sc, kk = scores_of(keys[block, 0], keys[block, 1])
        old = stat[0]
        top = jnp.maximum(old, jnp.max(sc, axis=1, keepdims=True))
        scale = jnp.exp(old - top)
        expo = jnp.exp(sc - top[:, :1])
        stat[0] = top
        stat[1] = stat[1] * scale + jnp.sum(expo, axis=1, keepdims=True)
        acc[...] = acc[...] * scale[:, :1] + jnp.dot(
            expo.astype(jnp.bfloat16), kk, preferred_element_type=jnp.float32
        )

    for r in range(2):
        pair(r).wait()
    mine = pl.ds(pl.multiple_of(s * part, part), part)
    sc, kk = scores_of(feats[0, mine, :], feats[1, mine, :])
    query = lax.broadcasted_iota(jnp.int32, sc.shape, 0)
    key = lax.broadcasted_iota(jnp.int32, sc.shape, 1) + s * part
    masked = query == key
    sc = jnp.where(masked, lowest, sc)
    top = jnp.max(sc, axis=1, keepdims=True)
    expo = jnp.where(masked, 0.0, jnp.exp(sc - top))
    stat[0] = jnp.broadcast_to(top, stat.shape[1:])
    stat[1] = jnp.broadcast_to(jnp.sum(expo, axis=1, keepdims=True), stat.shape[1:])
    acc[...] = jnp.dot(expo.astype(jnp.bfloat16), kk, preferred_element_type=jnp.float32)

    def from_z(k):
        block = slot(peer_of(z, k, blks), x)
        for h in range(2):
            arrived(block, h)
            repeat(tiles - 1, lambda j: forward(k, j, h).start())
        attend(block)

    def from_x(k):
        block = slot(z, peer_of(x, k, tiles))
        for h in range(2):
            arrived(block, h)
        attend(block)

    def diagonal(k):
        def one(j):
            block = slot(peer_of(z, k, blks), peer_of(x, j, tiles))
            for h in range(2):
                arrived(block, h)
            attend(block)
        repeat(tiles - 1, one)

    repeat(tiles - 1, from_x)
    repeat(blks - 1, from_z)
    repeat(blks - 1, diagonal)

    put_acc[...] = acc[...].astype(jnp.bfloat16)
    lane = lax.broadcasted_iota(jnp.int32, put_stat.shape, 1)
    put_stat[...] = jnp.where(lane < width // 2, stat[0], stat[1])
    send_acc = pltpu.make_async_remote_copy(
        put_acc, got_acc, part_send.at[0], part_recv.at[0],
        device_id={"sub": other}, device_id_type=MESH,
    )
    send_stat = pltpu.make_async_remote_copy(
        put_stat, got_stat, part_send.at[1], part_recv.at[1],
        device_id={"sub": other}, device_id_type=MESH,
    )
    send_stat.start()
    send_acc.start()

    def own_sent(k):
        for r in range(2):
            own_to_z(k, r).wait_send()

    def own_sent_x(k):
        for r in range(2):
            own_to_x(k, r).wait_send()

    def fwd_sent(k):
        def one(j):
            for h in range(2):
                forward(k, j, h).wait_send()
        repeat(tiles - 1, one)

    repeat(blks - 1, own_sent)
    repeat(tiles - 1, own_sent_x)
    repeat(blks - 1, fwd_sent)

    send_stat.wait()
    my_top, my_total = stat[0][:, :1], stat[1][:, :1]
    its_top, its_total = got_stat[:, :1], got_stat[:, width // 2:width // 2 + 1]
    top = jnp.maximum(my_top, its_top)
    mine_by, its_by = jnp.exp(my_top - top), jnp.exp(its_top - top)
    total = my_total * mine_by + its_total * its_by
    mine_by, its_by = mine_by / total, its_by / total
    send_acc.wait()
    gathered = acc[...] * mine_by + got_acc[...].astype(jnp.float32) * its_by
    whole = jnp.concatenate([feats[0], feats[1]], axis=1).astype(jnp.float32)
    mixed = whole + gathered
    squares = jnp.sum(mixed * mixed, axis=1, keepdims=True)
    wanted = jnp.where(s == 0, mixed[:, :width], mixed[:, width:])
    out_ref[...] = wanted * lax.rsqrt(squares + 1e-06)


def local(raw_desc, desc_mean, whitening):
    rows, depth = raw_desc.shape
    width = whitening.shape[1]
    blks, tiles = lax.axis_size("blk"), lax.axis_size("tile")
    chunks = 4
    part = rows // 2
    chips = blks * tiles
    vmem = pl.BlockSpec(memory_space=pltpu.VMEM)
    hbm = pl.BlockSpec(memory_space=pl.ANY)
    dma = pltpu.SemaphoreType.DMA
    bf16, f32 = jnp.bfloat16, jnp.float32
    return pl.pallas_call(
        functools.partial(kernel, blks, tiles, chunks),
        out_shape=jax.ShapeDtypeStruct((rows, width), f32),
        in_specs=[hbm, vmem, hbm],
        out_specs=vmem,
        scratch_shapes=[
            pltpu.VMEM((rows, depth), bf16),
            pltpu.VMEM((depth, width), bf16),
            pltpu.VMEM((2, rows, width), bf16),
            pltpu.VMEM((chips, 2, part, width), bf16),
            pltpu.VMEM((rows, 2 * width), f32),
            pltpu.VMEM((2, rows, width), f32),
            pltpu.VMEM((rows, 2 * width), bf16),
            pltpu.VMEM((rows, width), f32),
            pltpu.VMEM((rows, 2 * width), bf16),
            pltpu.VMEM((rows, width), f32),
            dma((chunks,)),
            dma,
            dma((2,)),
            dma((2,)),
            dma((blks - 1 + tiles - 1, 2)),
            dma((blks - 1, tiles - 1, 2)),
            dma((chips, 2)),
            dma((2,)),
            dma((2,)),
        ],
        compiler_params=pltpu.CompilerParams(collective_id=0, has_side_effects=True),
        name="augment",
    )(raw_desc, desc_mean, whitening)


def solution(mesh):
    return jax.shard_map(
        local,
        mesh=mesh,
        in_specs=(P(("groups", "blk", "tile"), None), P(), P(None, "sub")),
        out_specs=P(("groups", "blk", "tile"), "sub"),
        check_vma=False,
    )
```

time: 49.2 us -> 20.9 us (0.42)
  blocking collectives: 43.3 us -> 0 us
  Pallas kernels: 0 us -> 19.1 us
  matrix products: 2.86 us -> 0 us
  other arithmetic: 0.81 us -> 0 us
    all_gather x6 -> x0, blocking collectives: 40.8 us -> none  [the longest x3 15.8 us: merged_2(): everything = jax.tree.map(lambda part: lax.all_gather(part, axis), value)]
    pallas_call x0 -> x1, Pallas kernels: none -> 19.1 us  [local(): pl.pallas_call(functools.partial(kernel, blks, tiles, chunks), out_shape=...]
    dot_general x3 -> x0, matrix products: 2.86 us -> none  [the longest x1 1.51 us: local(): jnp.dot(centred, whitening, preferred_element_type=jnp.float32)]
    psum x1 -> x0, blocking collectives: 2.47 us -> none  [local(): squares = lax.psum(jnp.sum(mixed * mixed, axis=1), 'sub')]
    reduce_sum x2 -> x0, other arithmetic: 0.76 us -> none  [the longest x1 0.7 us: local(): total = jnp.sum(expo, axis=1)]
    mul x1 -> x0, local copies, waits for them, and re-layouts: 0.76 us -> none  [local(): return mixed * lax.rsqrt(squares + 1e-06)[:, None]]
    unnamed x2 -> x1, local copies, waits for them, and re-layouts: 0.98 us -> 1.57 us
where the time goes in v1:
time: 20.9 us; the launch traced here: 20.7 us
  Pallas kernels  19.1 us (91%)
  local copies, waits for them, and re-layouts  1.57 us (8%)
    pallas_call x1, Pallas kernels, local(): pl.pallas_call(functools.partial(kernel, blks, tiles, chunks), out_shape=...  19.1 us
    unnamed x1, local copies, waits for them, and re-layouts  1.57 us

profile of v1, /device:TPU:0, one launch (start us, length us, event | category | flops | bytes accessed | tf_op | source)
XLA Modules:
  0.0 20.7 jit_solution(10255362938372874136)
XLA Ops:
  0.0 19.1 %augment.1 = f32[256,128]{1,0:T(8,128)} custom-call(bf16[256,1536]{1,0:T(8,128)(2,1)} %raw_hbm.1, f32[1536]{0:T(1024)} %mean_ref.1, bf16[1536,128]{1,0:T(8,128)(2,1)} %white_hbm.1), custom_call_target="tpu_custom_call" | custom-call | tf_op jit(solution)/shard_map/augment/pallas_call | solution.py:243
  19.1 1.6 %copy.5 = f32[256,128]{1,0:T(8,128)} copy(f32[256,128]{1,0:T(8,128)} %augment.1) | data formatting | bytes 262144

commit v2 on v1

--- a/solution.py
+++ b/solution.py
@@ -237,9 +237,11 @@
     part = rows // 2
     chips = blks * tiles
     vmem = pl.BlockSpec(memory_space=pltpu.VMEM)
-    hbm = pl.BlockSpec(memory_space=pl.ANY)
+    hbm = pl.BlockSpec(memory_space=pltpu.HBM)
     dma = pltpu.SemaphoreType.DMA
     bf16, f32 = jnp.bfloat16, jnp.float32
+    raw_desc = pltpu.with_memory_space_constraint(raw_desc, pltpu.HBM)
+    whitening = pltpu.with_memory_space_constraint(whitening, pltpu.HBM)
     return pl.pallas_call(
         functools.partial(kernel, blks, tiles, chunks),
         out_shape=jax.ShapeDtypeStruct((rows, width), f32),
@@ -266,7 +268,7 @@
             dma((2,)),
             dma((2,)),
         ],
-        compiler_params=pltpu.CompilerParams(collective_id=0, has_side_effects=True),
+        compiler_params=pltpu.CompilerParams(collective_id=0, has_side_effects=True, vmem_limit_bytes=40 * 2 ** 20),
         name="augment",
     )(raw_desc, desc_mean, whitening)
 

time: 20.9 us -> 19.3 us (0.923)
  Pallas kernels: 19.1 us -> 17.8 us
  local copies, waits for them, and re-layouts: 1.57 us -> 1.35 us
    pallas_call x1, Pallas kernels: 19.1 us -> 17.8 us  [local(): pl.pallas_call(functools.partial(kernel, blks, tiles, chunks), out_shape=...]
    unnamed x1 -> x3, local copies, waits for them, and re-layouts: 1.57 us -> 1.35 us
where the time goes in v2:
time: 19.3 us; the launch traced here: 19.1 us
  Pallas kernels  17.8 us (92%)
  local copies, waits for them, and re-layouts  1.35 us (7%)
    pallas_call x1, Pallas kernels, local(): pl.pallas_call(functools.partial(kernel, blks, tiles, chunks), out_shape=...  17.8 us
    unnamed x3, local copies, waits for them, and re-layouts  1.35 us

profile of v2, /device:TPU:0, one launch (start us, length us, event | category | flops | bytes accessed | tf_op | source)
XLA Modules:
  0.0 19.1 jit_solution(12136667650400405090)
XLA Ops:
  0.0 0.0 copy-start
  0.0 0.7 %copy-done = f32[1536]{0:T(1024)S(1)} copy-done((f32[1536]{0:T(1024)S(1)}, f32[1536]{0:T(1024)}, u32[]{:S(2)}) %copy-start) | copy-done | bytes 6168
  0.7 17.8 %augment.1 = f32[256,128]{1,0:T(8,128)S(1)} custom-call(bf16[256,1536]{1,0:T(8,128)(2,1)} %raw_hbm.1, f32[1536]{0:T(1024)S(1)} %copy-done, bf16[1536,128]{1,0:T(8,128)(2,1)} %white_hbm.1), custom_call_target="tpu_custom_call" | custom-call | tf_op jit(solution)/shard_map/augment/pallas_call | solution.py:245
  18.5 0.7 %copy.5 = f32[256,128]{1,0:T(8,128)} copy(f32[256,128]{1,0:T(8,128)S(1)} %augment.1) | data formatting | bytes 262144
Async XLA Ops:
  0.0 0.7 %copy-start = (f32[1536]{0:T(1024)S(1)}, f32[1536]{0:T(1024)}, u32[]{:S(2)}) copy-start(f32[1536]{0:T(1024)} %mean_ref.1) | copy-start | bytes 18436
